TPU v7x, 32 devices: a whole 2x2x4 slice. The times are simulated.
32 devices in a mesh: subset: 8 (over z, x), vocab: 4 (over y, core).
Axes of the slice: x: 2, y: 2, z: 4, core: 2. Of those that a mesh axis runs over, the one named last changes fastest.
Arguments:
- hidden: bfloat16 [4096, 2048], P('subset', 'vocab'), may hold values from -100 to 100
- proj_weight: bfloat16 [2048, 25600], P('subset', 'vocab'), may hold values from -1 to 1
- targets: int32 [4096], P('subset'), may hold values from 0 to 25599
- counts: int32 [8, 100, 512], P('subset', 'vocab'), may hold values from 1 to 15, as said below
- ranks: int32 [8], replicated, may hold values from 0 to 799
Outputs:
- row_cross_entropy: float32 [4096], P('subset')
- resample_mean_losses: float32 [8, 100], P('subset', 'vocab')
- quantiles: float32 [8], replicated
Inputs may be any that keep to these rules, and one draw needn't show every extreme that they name: For every subset and resample the counts over the 512 rows sum to 4096.
All inputs are finite; a program needn't handle non-finite values.
Results may differ from a plain program's by a relative error of at most 0.0003.
Values may be sent and summed in bfloat16 or wider, within the bound.
No kernel may reach another device: no remote copies, remote signals or barrier semaphores. Data moves between devices by JAX's collectives and lax.ppermute only.
A program may use at most 128 MiB of HBM per device.

v0:
```python
import jax
import jax.numpy as jnp
from jax import lax
from jax.sharding import PartitionSpec as P


def shards(hidden, proj_weight, targets, counts, ranks):
    features = lax.all_gather(hidden, "vocab", axis=1, tiled=True)
    columns = proj_weight.shape[1]
    whole_weight = lax.all_gather(proj_weight, "subset", axis=0, tiled=True)
    logit_scores = jnp.dot(features, whole_weight, preferred_element_type=jnp.float32)
    local_top = jnp.max(logit_scores, axis=1)
    local_sum = jnp.sum(jnp.exp(logit_scores - local_top[:, None]), axis=1)
    offset = targets - lax.axis_index("vocab") * columns
    inside = (offset >= 0) & (offset < columns)
    picked = jnp.take_along_axis(logit_scores, jnp.clip(offset, 0, columns - 1)[:, None], axis=1)[
        :, 0
    ]
    picked = jnp.where(inside, picked, 0.0)
    row_max = lax.pmax(local_top, "vocab")
    row_total, target_logit = lax.psum((local_sum * jnp.exp(local_top - row_max), picked), "vocab")
    row_cross_entropy = row_max + jnp.log(row_total) - target_logit
    total_rows = 1.0 * lax.axis_size("subset") * row_cross_entropy.shape[0]
    resample_mean_losses = (
        jnp.einsum(
            "cno,o->cn",
            counts.astype(jnp.float32),
            row_cross_entropy,
            precision=lax.Precision.HIGHEST,
        )
        / total_rows
    )
    grouped = lax.all_gather(resample_mean_losses, "vocab", axis=1, tiled=True)
    gathered = lax.all_gather(grouped, "subset", axis=0, tiled=True)
    pooled = jnp.sort(gathered.reshape(-1))
    positions = lax.iota(jnp.int32, pooled.shape[0])
    chosen = positions[:, None] == ranks[None, :]
    quantiles = jnp.sum(jnp.where(chosen, pooled[:, None], 0.0), axis=0)
    return (row_cross_entropy, resample_mean_losses, quantiles)


def solution(mesh):
    return jax.shard_map(
        shards,
        mesh=mesh,
        in_specs=(
            P("subset", "vocab"),
            P("subset", "vocab"),
            P("subset"),
            P("subset", "vocab", None),
            P(),
        ),
        out_specs=(P("subset"), P("subset", "vocab"), P()),
        check_vma=False,
    )
```

profile of v0, /device:TPU:0, one launch (start us, length us, event | category | flops | bytes accessed | tf_op | source)
XLA Modules:
  0.0 625.1 jit_solution(13795552494358012324)
XLA Ops:
  7.2 0.0 all-gather.5.cloned.1.call-start
  7.2 0.7 all-gather.5.cloned.1.call-update
  7.9 0.0 all-gather.7.cloned.1.call-start
  7.9 0.7 all-gather.7.cloned.1.call-update
  8.7 0.8 convert_element_type.3
  9.5 1.2 dynamic-slice
  10.8 1.2 dynamic-slice.1
  13.3 0.7 compare_select_fusion
  14.0 20.8 %all-gather.5.cloned.1.call-done = bf16[512,2048]{1,0:T(8,128)(2,1)} async-done(((bf16[512,512]{1,0:T(8,128)(2,1)}), bf16[512,2048]{1,0:T(8,128)(2,1)}) %all-gather.5.cloned.1.call-update) | async-done | bytes 2097168 | tf_op jit(solution)/shard_map/all_gather | solution.py:8
  34.9 501.6 %all-gather.7.cloned.1.call-done = bf16[2048,6400]{1,0:T(8,128)(2,1)} async-done(((bf16[256,6400]{1,0:T(8,128)(2,1)}), bf16[2048,6400]{1,0:T(8,128)(2,1)}) %all-gather.7.cloned.1.call-update) | async-done | bytes 26214416 | tf_op jit(solution)/shard_map/all_gather | solution.py:10
  536.4 22.5 %fusion.6 = (f32[512]{0:T(512)S(1)}, f32[512,6400]{1,0:T(8,128)}) fusion(bf16[512,2048]{1,0:T(8,128)(2,1)} %all-gather.5.cloned.1.call-done, bf16[2048,6400]{1,0:T(8,128)(2,1)} %all-gather.7.cloned.1.call-done), kind=kOutput, calls=%fused_computation.18 | convolution fusion | flops 13425049600 | bytes 41420800 | tf_op jit(solution)/shard_map/dot_general | solution.py:11
  558.9 0.0 copy-start
  558.9 0.0 copy-start.3
  558.9 6.5 %pmax.7 = f32[512]{0:T(512)S(1)} all-reduce(f32[512]{0:T(512)S(1)} %get-tuple-element.8), channel_id=1, replica_groups=mesh['subset'=8,'vocab'=4] {'vocab'}, use_global_device_ids=true, to_apply=%region_1.0 | all-reduce | flops 512 | bytes 4096 | tf_op jit(solution)/shard_map/pmax | solution.py:20
  565.5 6.6 %exponential_reduce_fusion = f32[512]{0:T(512)S(1)} fusion(f32[512,6400]{1,0:T(8,128)} %get-tuple-element.9, f32[512]{0:T(512)S(1)} %get-tuple-element.8), kind=kLoop, calls=%fused_computation.1 | loop fusion | flops 6553088 | bytes 13111296 | tf_op jit(solution)/shard_map/reduce_sum | solution.py:13
  572.0 8.2 %gather_fusion = f32[512]{0:T(512)S(1)} fusion(f32[512,6400]{1,0:T(8,128)} %get-tuple-element.9, s32[512]{0:T(512)S(1)} %bitcast.18), kind=kCustom, calls=%fused_computation | custom fusion | bytes 8192 | tf_op jit(solution)/shard_map/jit(take_along_axis)/gather | solution.py:16
  580.2 0.0 copy-done
  580.2 5.8 all-reduce.2
  586.1 0.0 copy-start.1
  586.1 0.1 fusion
  586.2 0.0 copy-start.2
  586.3 0.2 dynamic-update-slice
  586.5 5.7 all-reduce
  592.3 0.2 dynamic-update-slice.1
  592.5 20.5 %all-reduce.1 = f32[800]{0:T(1024)S(1)} all-reduce(f32[800]{0:T(1024)S(1)} %dynamic-update-slice.1), channel_id=3, replica_groups=mesh['subset'=8,'vocab'=4] {'subset'}, use_global_device_ids=true, to_apply=%add.1 | all-reduce | flops 800 | bytes 6400
  613.0 4.5 sort.15
  617.5 0.0 copy-done.3
  617.6 0.7 select_reduce_fusion
  618.3 0.0 copy-done.1
  618.3 0.0 copy-done.2
  (9 shorter events, 0.1 us)
Async XLA Ops:
  7.2 27.7 %all-gather.5.cloned.1.call-start = ((), (), s32[]{:S(2)}) async-start(), calls=%async_computation | async-start | bytes 2621440 | tf_op jit(solution)/shard_map/all_gather | solution.py:8
  7.9 528.6 %all-gather.7.cloned.1.call-start = ((), (), s32[]{:S(2)}) async-start(), calls=%async_computation.1 | async-start | bytes 29491200 | tf_op jit(solution)/shard_map/all_gather | solution.py:10
  558.9 21.3 %copy-start = (s32[512]{0:T(512)S(1)}, s32[512]{0:T(512)}, u32[]{:S(2)}) copy-start(s32[512]{0:T(512)} %param.7) | copy-start | bytes 6148
  558.9 58.6 %copy-start.3 = (s32[8]{0:T(128)S(1)}, s32[8]{0:T(128)}, u32[]{:S(2)}) copy-start(s32[8]{0:T(128)} %param.9) | copy-start | bytes 100
  586.1 32.2 %copy-start.1 = (f32[512]{0:T(512)}, f32[512]{0:T(512)S(1)}, u32[]{:S(2)}) copy-start(f32[512]{0:T(512)S(1)} %add_subtract_fusion) | copy-start | bytes 6148
  586.2 32.0 %copy-start.2 = (f32[25]{0:T(128)}, f32[25]{0:T(128)S(1)}, u32[]{:S(2)}) copy-start(f32[25]{0:T(128)S(1)} %fusion) | copy-start | bytes 304
Sparse Core Ops, SparseCore 0:
  9.5 25.2 all-gather.4
  36.4 500.0 all-gather.6
where the time goes:
time: 626 us; the launch traced here: 625 us
  waiting for transfers between devices  524 us (84%)
  blocking collectives  38.6 us (6%)
  matrix products  22.6 us (4%)
  between operations  15.4 us (2%)
  other arithmetic  13.4 us (2%)
  local copies, waits for them, and re-layouts  11.1 us (2%)
    all_gather x1, waiting for transfers between devices, shards(): whole_weight = lax.all_gather(proj_weight, 'subset', axis=0, tiled=True)  502 us
    unnamed x2, blocking collectives  26.3 us
    dot_general x1, matrix products, shards(): jnp.dot(features, whole_weight, preferred_element_type=jnp.float32)  22.5 us
    all_gather x1, waiting for transfers between devices, shards(): features = lax.all_gather(hidden, 'vocab', axis=1, tiled=True)  20.8 us
  transfers between devices with their start and end apart: 2, of which 2 were waited for; matrix products, arithmetic and copies ran while one was open for 1% of the time, Pallas kernels for 0%

commit v1 on v0

--- a/solution.py
+++ b/solution.py
@@ -7,7 +7,9 @@
 def shards(hidden, proj_weight, targets, counts, ranks):
     features = lax.all_gather(hidden, "vocab", axis=1, tiled=True)
     columns = proj_weight.shape[1]
-    whole_weight = lax.all_gather(proj_weight, "subset", axis=0, tiled=True)
+    whole_weight = jnp.concatenate(
+        lax.all_to_all(jnp.stack([proj_weight] * lax.axis_size("subset")), "subset", 0, 0), axis=0
+    )
     logit_scores = jnp.dot(features, whole_weight, preferred_element_type=jnp.float32)
     local_top = jnp.max(logit_scores, axis=1)
     local_sum = jnp.sum(jnp.exp(logit_scores - local_top[:, None]), axis=1)

time: 626 us -> 679 us (1.085)
  waiting for transfers between devices: 524 us -> 564 us
  local copies, waits for them, and re-layouts: 11.1 us -> 19.7 us
  starting transfers between devices: 0.08 us -> 7.46 us
    all_to_all x0 -> x1, waiting for transfers between devices: none -> 540 us  [shards(): lax.all_to_all(jnp.stack([proj_weight] * lax.axis_size('subset')), 'subse...]
    all_gather x1 -> x0, waiting for transfers between devices: 502 us -> none  [shards(): whole_weight = lax.all_gather(proj_weight, 'subset', axis=0, tiled=True)]
    another operation x1 -> x2, local copies, waits for them, and re-layouts: 0.01 us -> 9.85 us  [the longest x1 9.85 us: shards(): jnp.stack([proj_weight] * lax.axis_size('subset'))]
    all_to_all x0 -> x1, starting transfers between devices: none -> 7.42 us  [shards(): lax.all_to_all(jnp.stack([proj_weight] * lax.axis_size('subset')), 'subse...]
  transfers between devices with their start and end apart: 2 -> 2, of which waited for: 2 -> 2; matrix products, arithmetic and copies ran while one was open for 1% -> 0% of each run, Pallas kernels for 0% -> 0%
where the time goes in v1:
time: 679 us; the launch traced here: 678 us
  waiting for transfers between devices  564 us (83%)
  blocking collectives  37.1 us (5%)
  matrix products  22.6 us (3%)
  local copies, waits for them, and re-layouts  19.7 us (3%)
  between operations  15.5 us (2%)
  other arithmetic  11.9 us (2%)
  starting transfers between devices  7.46 us (1%)
    all_to_all x1, waiting for transfers between devices, shards(): lax.all_to_all(jnp.stack([proj_weight] * lax.axis_size('subset')), 'subse...  540 us
    unnamed x2, blocking collectives  25.3 us
    all_gather x1, waiting for transfers between devices, shards(): features = lax.all_gather(hidden, 'vocab', axis=1, tiled=True)  23.7 us
    dot_general x1, matrix products, shards(): jnp.dot(features, whole_weight, preferred_element_type=jnp.float32)  22.5 us
  transfers between devices with their start and end apart: 2, of which 2 were waited for; matrix products, arithmetic and copies ran while one was open for 0% of the time, Pallas kernels for 0%

profile of v1, /device:TPU:0, one launch (start us, length us, event | category | flops | bytes accessed | tf_op | source)
XLA Modules:
  0.0 678.1 jit_solution(13325294804173188870)
XLA Ops:
  7.2 9.8 %stack.2 = bf16[8,256,6400]{2,1,0:T(8,128)(2,1)} broadcast(bf16[256,6400]{1,0:T(8,128)(2,1)} %param.6), dimensions={1,2} | broadcast | bytes 29491200 | tf_op jit(solution)/shard_map/stack | solution.py:11
  17.0 0.0 copy-start
  17.0 0.0 copy-start.6
  17.0 0.0 copy-start.5
  17.0 0.0 copy-start.1
  17.0 7.4 %all-to-all-start = ((bf16[8,256,6400]{2,1,0:T(8,128)(2,1)}), bf16[8,256,6400]{2,1,0:T(8,128)(2,1)}, u32[]{:S(2)}, u32[]{:S(2)}) async-start(bf16[8,256,6400]{2,1,0:T(8,128)(2,1)} %stack.2), calls=%async_computation | async-start | bytes 52428800 | tf_op jit(solution)/shard_map/all_to_all | solution.py:11
  24.5 0.0 all-gather.4.cloned.1.call-start
  24.5 0.7 all-gather.4.cloned.1.call-update
  25.2 0.0 copy-done
  25.3 0.0 copy-done.6
  25.3 0.6 dynamic-slice
  25.9 0.0 copy-done.5
  25.9 0.6 dynamic-slice.1
  27.8 0.0 copy-done.1
  27.8 23.7 %all-gather.4.cloned.1.call-done = bf16[512,2048]{1,0:T(8,128)(2,1)} async-done(((bf16[512,512]{1,0:T(8,128)(2,1)}), bf16[512,2048]{1,0:T(8,128)(2,1)}) %all-gather.4.cloned.1.call-update) | async-done | bytes 2097168 | tf_op jit(solution)/shard_map/all_gather | solution.py:8
  51.5 539.5 %all-to-all-done = bf16[8,256,6400]{2,1,0:T(8,128)(2,1)} async-done(((bf16[8,256,6400]{2,1,0:T(8,128)(2,1)}), bf16[8,256,6400]{2,1,0:T(8,128)(2,1)}, u32[]{:S(2)}, u32[]{:S(2)}) %all-to-all-start) | async-done | bytes 26214432 | tf_op jit(solution)/shard_map/all_to_all | solution.py:11
  591.0 22.5 %fusion.6 = (f32[512]{0:T(512)S(1)}, f32[512,6400]{1,0:T(8,128)}) fusion(bf16[512,2048]{1,0:T(8,128)(2,1)} %all-gather.4.cloned.1.call-done, bf16[2048,6400]{1,0:T(8,128)(2,1)} %bitcast), kind=kOutput, calls=%fused_computation.18 | convolution fusion | flops 13425049600 | bytes 41420800 | tf_op jit(solution)/shard_map/dot_general | solution.py:13
  613.5 0.0 copy-start.4
  613.5 5.6 pmax.7
  619.2 6.6 exponential_reduce_fusion
  625.7 8.2 %gather_fusion = f32[512]{0:T(512)S(1)} fusion(f32[512,6400]{1,0:T(8,128)} %get-tuple-element.9, s32[512]{0:T(512)S(1)} %bitcast.19), kind=kCustom, calls=%fused_computation | custom fusion | bytes 8192 | tf_op jit(solution)/shard_map/jit(take_along_axis)/gather | solution.py:18
  633.9 6.1 all-reduce.2
  640.1 0.0 copy-start.2
  640.1 0.1 fusion
  640.2 0.0 copy-start.3
  640.2 0.2 dynamic-update-slice
  640.5 5.8 all-reduce
  646.3 0.2 dynamic-update-slice.1
  646.5 19.5 %all-reduce.1 = f32[800]{0:T(1024)S(1)} all-reduce(f32[800]{0:T(1024)S(1)} %dynamic-update-slice.1), channel_id=3, replica_groups=mesh['subset'=8,'vocab'=4] {'subset'}, use_global_device_ids=true, to_apply=%add.1 | all-reduce | flops 800 | bytes 6400
  666.0 4.5 sort.15
  670.6 0.0 copy-done.4
  670.6 0.7 select_reduce_fusion
  671.3 0.0 copy-done.2
  671.3 0.0 copy-done.3
  (11 shorter events, 0.1 us)
Async XLA Ops:
  17.0 8.2 %copy-start = (s32[1,25,512]{2,0,1:T(1,128)S(1)}, s32[1,25,512]{2,0,1:T(1,128)}, u32[]{:S(2)}) copy-start(s32[1,25,512]{2,0,1:T(1,128)} %param.8) | copy-start | bytes 153604
  17.0 8.3 %copy-start.6 = (u32[32]{0:T(128)S(1)}, u32[32]{0:T(128)}, u32[]{:S(2)}) copy-start(u32[32]{0:T(128)} %constant.61) | copy-start | bytes 388
  17.0 8.9 %copy-start.5 = (u32[32]{0:T(128)S(1)}, u32[32]{0:T(128)}, u32[]{:S(2)}) copy-start(u32[32]{0:T(128)} %constant.66) | copy-start | bytes 388
  17.0 10.7 %copy-start.1 = (s32[512]{0:T(512)S(1)}, s32[512]{0:T(512)}, u32[]{:S(2)}) copy-start(s32[512]{0:T(512)} %param.7) | copy-start | bytes 6148
  17.0 574.0 %all-to-all-start = ((bf16[8,256,6400]{2,1,0:T(8,128)(2,1)}), bf16[8,256,6400]{2,1,0:T(8,128)(2,1)}, u32[]{:S(2)}, u32[]{:S(2)}) async-start(bf16[8,256,6400]{2,1,0:T(8,128)(2,1)} %stack.2), calls=%async_computation | async-start | bytes 52428800 | tf_op jit(solution)/shard_map/all_to_all | solution.py:11
  24.5 27.0 %all-gather.4.cloned.1.call-start = ((), (), s32[]{:S(2)}) async-start(), calls=%async_computation.1 | async-start | bytes 2621440 | tf_op jit(solution)/shard_map/all_gather | solution.py:8
  613.5 57.0 %copy-start.4 = (s32[8]{0:T(128)S(1)}, s32[8]{0:T(128)}, u32[]{:S(2)}) copy-start(s32[8]{0:T(128)} %param.9) | copy-start | bytes 100
  640.1 31.2 %copy-start.2 = (f32[512]{0:T(512)}, f32[512]{0:T(512)S(1)}, u32[]{:S(2)}) copy-start(f32[512]{0:T(512)S(1)} %add_subtract_fusion) | copy-start | bytes 6148
  640.2 31.1 %copy-start.3 = (f32[25]{0:T(128)}, f32[25]{0:T(128)S(1)}, u32[]{:S(2)}) copy-start(f32[25]{0:T(128)S(1)} %fusion) | copy-start | bytes 304
Sparse Core Ops, SparseCore 0:
  26.8 24.5 all-gather.3
